TPU v7x, 32 devices: a whole 2x2x4 slice. The times are simulated.
32 devices in a mesh: dp: 2 (over x), row: 4 (over z), col: 4 (over y, core).
Axes of the slice: x: 2, y: 2, z: 4, core: 2. Of those that a mesh axis runs over, the one named last changes fastest.
Arguments:
- expand_gradient: bfloat16 [2, 4096, 5120], P('dp', 'row', 'col'), may hold values from -24 to 24, as said below
- expand_master: float32 [4096, 5120], P(('row', 'dp'), 'col'), may hold values from -0.12 to 0.12
- expand_rows: float32 [4096], P(('row', 'dp')), may hold values from 0.01 to 1
- expand_columns: float32 [5120], P('col'), may hold values from 0.01 to 1
- contract_gradient: bfloat16 [2, 5120, 4096], P('dp', 'row', 'col'), may hold values from -24 to 24, as said below
- contract_master: float32 [5120, 4096], P(('row', 'dp'), 'col'), may hold values from -0.12 to 0.12
- contract_rows: float32 [5120], P(('row', 'dp')), may hold values from 0.01 to 1
- contract_columns: float32 [4096], P('col'), may hold values from 0.01 to 1
- attend_gradient: bfloat16 [2, 4096, 4096], P('dp', 'row', 'col'), may hold values from -24 to 24, as said below
- attend_master: float32 [4096, 4096], P(('row', 'dp'), 'col'), may hold values from -0.12 to 0.12
- attend_rows: float32 [4096], P(('row', 'dp')), may hold values from 0.01 to 1
- attend_columns: float32 [4096], P('col'), may hold values from 0.01 to 1
Outputs:
- expand_updated: float32 [4096, 5120], P(('row', 'dp'), 'col')
- expand_weights: bfloat16 [4096, 5120], P('row', 'col')
- expand_rows_next: float32 [4096], P(('row', 'dp'))
- expand_columns_next: float32 [5120], P('col')
- expand_step: float32 [4096, 5120], P(('row', 'dp'), 'col')
- contract_updated: float32 [5120, 4096], P(('row', 'dp'), 'col')
- contract_weights: bfloat16 [5120, 4096], P('row', 'col')
- contract_rows_next: float32 [5120], P(('row', 'dp'))
- contract_columns_next: float32 [4096], P('col')
- contract_step: float32 [5120, 4096], P(('row', 'dp'), 'col')
- attend_updated: float32 [4096, 4096], P(('row', 'dp'), 'col')
- attend_weights: bfloat16 [4096, 4096], P('row', 'col')
- attend_rows_next: float32 [4096], P(('row', 'dp'))
- attend_columns_next: float32 [4096], P('col')
- attend_step: float32 [4096, 4096], P(('row', 'dp'), 'col')
Inputs may be any that keep to these rules, and one draw needn't show every extreme that they name: `expand_gradient`: each replica's gradient, of any scale from entry to entry. `contract_gradient`: each replica's gradient, of any scale from entry to entry. `attend_gradient`: each replica's gradient, of any scale from entry to entry.
All inputs are finite; a program needn't handle non-finite values.
Results may differ from a plain program's by a relative error of at most 0.0004.
Values may be sent and summed in bfloat16 or wider, within the bound.
A program may use at most 128 MiB of HBM per device.

v0:
```python
import jax
import jax.numpy as jnp
from jax import lax
from jax.sharding import PartitionSpec as P

tiny_square = 1e-30
decay_rate = 0.9
learn_rate = 0.01


def finish(update_raw, clip_total, master, full_size):
    clip_scale = jnp.maximum(1.0, jnp.sqrt(clip_total / full_size))
    step_taken = update_raw / clip_scale
    updated = master - learn_rate * step_taken
    weights = lax.all_gather(updated.astype(jnp.bfloat16), "dp", axis=0, tiled=True)
    return (updated, weights, step_taken)


def reduce_gradient(gradient, dp_count):
    received = lax.all_to_all(gradient, "dp", split_axis=1, concat_axis=0, tiled=True)
    summed = jnp.sum(received.astype(jnp.float32), axis=0)
    return summed / dp_count


def body(
    expand_gradient,
    expand_master,
    expand_rows,
    expand_columns,
    contract_gradient,
    contract_master,
    contract_rows,
    contract_columns,
    attend_gradient,
    attend_master,
    attend_rows,
    attend_columns,
):
    groups = (
        (expand_gradient, expand_master, expand_rows, expand_columns),
        (contract_gradient, contract_master, contract_rows, contract_columns),
        (attend_gradient, attend_master, attend_rows, attend_columns),
    )
    dp_count = lax.axis_size("dp")
    col_count = lax.axis_size("col")
    split_count = dp_count * lax.axis_size("row")
    means = []
    for gradient, master, row_stat, column_stat in groups:
        means.append(reduce_gradient(gradient, dp_count))
    squares = [mean_grad * mean_grad + tiny_square for mean_grad in means]
    row_parts = [jnp.sum(square_block, axis=1) for square_block in squares]
    column_parts = [jnp.sum(square_block, axis=0) for square_block in squares]
    heights = [mean_grad.shape[0] * split_count for mean_grad in means]
    widths = [mean_grad.shape[1] * col_count for mean_grad in means]
    outputs = []
    for which in range(3):
        row_total = lax.psum(row_parts[which], "col")
        rows_next = decay_rate * groups[which][2] + (1.0 - decay_rate) * row_total / widths[which]
        column_total, rows_sum = lax.psum((column_parts[which], jnp.sum(rows_next)), ("dp", "row"))
        columns_next = (
            decay_rate * groups[which][3] + (1.0 - decay_rate) * column_total / heights[which]
        )
        row_mean = rows_sum / heights[which]
        update_raw = means[which] * jnp.sqrt(
            row_mean / (rows_next[:, None] * columns_next[None, :])
        )
        clip_total = lax.psum(jnp.sum(update_raw * update_raw), ("dp", "row", "col"))
        updated, weights, step_taken = finish(
            update_raw, clip_total, groups[which][1], heights[which] * widths[which]
        )
        outputs.extend([updated, weights, rows_next, columns_next, step_taken])
    return tuple(outputs)


def solution(mesh):
    return jax.shard_map(
        body,
        mesh=mesh,
        in_specs=(
            P("dp", "row", "col"),
            P(("row", "dp"), "col"),
            P(("row", "dp")),
            P("col"),
            P("dp", "row", "col"),
            P(("row", "dp"), "col"),
            P(("row", "dp")),
            P("col"),
            P("dp", "row", "col"),
            P(("row", "dp"), "col"),
            P(("row", "dp")),
            P("col"),
        ),
        out_specs=(
            P(("row", "dp"), "col"),
            P("row", "col"),
            P(("row", "dp")),
            P("col"),
            P(("row", "dp"), "col"),
            P(("row", "dp"), "col"),
            P("row", "col"),
            P(("row", "dp")),
            P("col"),
            P(("row", "dp"), "col"),
            P(("row", "dp"), "col"),
            P("row", "col"),
            P(("row", "dp")),
            P("col"),
            P(("row", "dp"), "col"),
        ),
        check_vma=False,
    )
```

profile of v0, /device:TPU:0, one launch (start us, length us, event | category | flops | bytes accessed | tf_op | source)
XLA Modules:
  0.0 387.2 jit_solution(6910142270513207531)
XLA Ops:
  7.2 6.8 %copy.41 = bf16[1,1024,1024]{2,0,1:T(2,128)(2,1)} copy(bf16[1,1024,1024]{2,1,0:T(8,128)(2,1)} %param.20) | data formatting | bytes 4194304 | tf_op args[8]
  13.9 0.5 broadcast.37
  14.4 12.8 %reduce.2 = bf16[1024,1024]{1,0:T(8,128)(2,1)S(1)} reduce(bf16[1024,1,1024]{2,1,0:T(2,128)(2,1)} %bitcast.22, bf16[]{:T(256)} %broadcast.37), dimensions={1}, to_apply=%bitcast.17.reduce_sub_computation | reduce | bytes 4194306
  27.2 2.5 reshape.58
  29.7 5.5 %all-to-all-start.2 = ((bf16[2,2,262144]{2,1,0:T(2,128)(2,1)}), bf16[2,2,262144]{2,1,0:T(2,128)(2,1)}, u32[]{:S(2)}, u32[]{:S(2)}) async-start(bf16[2,2,262144]{2,1,0:T(2,128)(2,1)} %reshape.58), calls=%async_computation.2 | async-start | bytes 4194304 | tf_op jit(solution)/shard_map/all_to_all | solution.py:20
  35.2 6.4 %copy.40 = bf16[1,1024,1280]{2,0,1:T(2,128)(2,1)} copy(bf16[1,1024,1280]{2,1,0:T(8,128)(2,1)S(1)} %copy-done.4) | data formatting | bytes 5242880 | tf_op args[0]
  41.6 26.6 %reduce = bf16[1024,1280]{1,0:T(8,128)(2,1)S(1)} reduce(bf16[1024,1,1280]{2,1,0:T(2,128)(2,1)} %bitcast.21, bf16[]{:T(256)} %broadcast.37), dimensions={1}, to_apply=%bitcast.16.reduce_sub_computation | reduce | bytes 5242882
  68.2 1.8 reshape.54
  70.0 5.8 %all-to-all-start = ((bf16[2,2,327680]{2,1,0:T(2,128)(2,1)}), bf16[2,2,327680]{2,1,0:T(2,128)(2,1)}, u32[]{:S(2)}, u32[]{:S(2)}) async-start(bf16[2,2,327680]{2,1,0:T(2,128)(2,1)} %reshape.54), calls=%async_computation | async-start | bytes 5242880 | tf_op jit(solution)/shard_map/all_to_all | solution.py:20
  75.9 18.2 %copy.39 = bf16[1,1280,1024]{2,0,1:T(2,128)(2,1)} copy(bf16[1,1280,1024]{2,1,0:T(8,128)(2,1)S(1)} %copy-done.5) | data formatting | bytes 5242880 | tf_op args[4]
  94.1 15.6 %reduce.1 = bf16[1280,1024]{1,0:T(8,128)(2,1)S(1)} reduce(bf16[1280,1,1024]{2,1,0:T(2,128)(2,1)} %bitcast.18, bf16[]{:T(256)} %broadcast.37), dimensions={1}, to_apply=%bitcast.15.reduce_sub_computation | reduce | bytes 5242882
  109.6 3.0 reshape.56
  112.6 4.1 %all-to-all-start.1 = ((bf16[2,2,327680]{2,1,0:T(2,128)(2,1)}), bf16[2,2,327680]{2,1,0:T(2,128)(2,1)S(1)}, u32[]{:S(2)}, u32[]{:S(2)}) async-start(bf16[2,2,327680]{2,1,0:T(2,128)(2,1)} %reshape.56), calls=%async_computation.1 | async-start | bytes 5242880 | tf_op jit(solution)/shard_map/all_to_all | solution.py:20
  116.8 0.2 all-gather.8.cloned.1.call-start
  116.9 4.3 %reshape.59 = bf16[1024,1,1024]{2,1,0:T(2,128)(2,1)} reshape(bf16[2,2,262144]{2,1,0:T(2,128)(2,1)} %all-to-all-done.2) | data formatting | bytes 4194304
  121.2 3.0 copy.35
  124.2 0.4 convert_reduce_fusion.2
  124.7 0.0 copy-start.1
  124.7 1.3 copy-done.1
  126.0 0.5 fusion.5
  126.5 5.1 %reshape.55 = bf16[1024,1,1280]{2,1,0:T(2,128)(2,1)} reshape(bf16[2,2,327680]{2,1,0:T(2,128)(2,1)} %all-to-all-done) | data formatting | bytes 5242880
  131.5 2.9 copy.31
  134.4 0.5 convert_reduce_fusion.1
  134.9 0.0 copy-start
  134.9 1.5 copy-done
  136.4 0.6 fusion.1
  137.0 11.3 %all-to-all-done.1 = bf16[2,2,327680]{2,1,0:T(2,128)(2,1)S(1)} async-done(((bf16[2,2,327680]{2,1,0:T(2,128)(2,1)}), bf16[2,2,327680]{2,1,0:T(2,128)(2,1)S(1)}, u32[]{:S(2)}, u32[]{:S(2)}) %all-to-all-start.1) | async-done | bytes 2621472 | tf_op jit(solution)/shard_map/all_to_all | solution.py:20
  148.3 3.7 reshape.57
  152.1 3.5 copy.33
  155.6 0.6 convert_reduce_fusion
  156.2 0.0 copy-start.14
  156.2 0.0 copy-start.17
  156.2 0.0 copy-start.18
  156.2 0.0 copy-start.13
  156.2 0.0 copy-start.15
  156.2 0.0 copy-start.16
  156.2 0.5 fusion.3
  156.8 6.2 %all-reduce.2 = (f32[512]{0:T(512)S(1)}, f32[640]{0:T(1024)S(1)}, f32[512]{0:T(512)S(1)}) all-reduce(f32[512]{0:T(512)S(1)} %get-tuple-element.17, f32[640]{0:T(1024)S(1)} %get-tuple-element.15, f32[512]{0:T(512)S(1)} %get-tuple-element.19), channel_id=1, replica_groups=mesh['dp'=2,'row'=4,'col'=4] {'col'}, use_global_device_ids=true, to_apply=%region_2.0 | all-reduce | flops 1664 | bytes 13312 | tf_op jit(solution)/shard_map/psum | solution.py:57
  163.0 0.6 fusion.10
  163.6 0.6 fusion.9
  164.2 38.0 %all-reduce.1 = (f32[1280]{0:T(1024)S(1)}, f32[]{:T(128)}, f32[1024]{0:T(1024)S(1)}, f32[]{:T(128)}, f32[1024]{0:T(1024)S(1)}, /*index=5*/f32[]{:T(128)}) all-reduce(f32[1280]{0:T(1024)S(1)} %get-tuple-element.18, f32[]{:T(128)} %get-tuple-element.48, ...), channel_id=1, replica_groups=mesh['dp'=2,'row'=4,'col'=4] {'dp','row'}, use_global_device_ids=true, to_apply=%region_6.0 | all-reduce | flops 3331 | bytes 26648 | tf_op jit(solution)/shard_map/psum | solution.py:59
  203.5 0.0 copy-start.7
  203.5 0.0 copy-start.10
  204.2 0.0 copy-start.8
  204.2 0.0 copy-start.2
  204.2 3.8 multiply_reduce_fusion.1
  208.0 2.3 multiply_reduce_fusion
  210.3 2.0 multiply_reduce_fusion.2
  212.2 37.2 %all-reduce = (f32[]{:T(128)}, f32[]{:T(128)}, f32[]{:T(128)}) all-reduce(f32[]{:T(128)} %multiply_reduce_fusion.1, f32[]{:T(128)} %multiply_reduce_fusion, f32[]{:T(128)} %multiply_reduce_fusion.2), channel_id=1, replica_groups=mesh['dp'=2,'row'=4,'col'=4] {'dp','row','col'}, use_global_device_ids=true, to_apply=%region_8.0 | all-reduce | flops 3 | bytes 24 | tf_op jit(solution)/shard_map/psum | solution.py:67
  250.2 5.9 %fusion.6 = (bf16[512,1024]{1,0:T(8,128)(2,1)}, f32[512,1024]{1,0:T(8,128)}, f32[512,1024]{1,0:T(8,128)}) fusion(f32[512,1024]{1,0:T(8,128)} %param.21, f32[]{:T(128)S(6)} %max.11, f32[1024]{0:T(1024)S(1)} %multiply_add_fusion.4, f32[512]{0:T(512)S(1)} %get-tuple-element.77, f32[]{:T(128)S(6)} %div.136, f32[512,1024]{1,0:T(8,128)} %copy-done.1), kind=kLoop, calls=%fused_computation.30 | loop fusion | flops 4194304 | bytes 9443336 | tf_op jit(solution)/shard_map/convert_element_type | solution.py:15
  256.1 0.0 all-gather.8.cloned.1.call-update
  256.1 0.0 all-gather.4.cloned.1.call-start
  256.9 6.7 %fusion.8 = (bf16[512,1280]{1,0:T(8,128)(2,1)}, f32[512,1280]{1,0:T(8,128)}, f32[512,1280]{1,0:T(8,128)}) fusion(f32[512,1280]{1,0:T(8,128)} %param.13, f32[]{:T(128)S(6)} %max.9, f32[1280]{0:T(1024)S(1)} %multiply_add_fusion.3, f32[512]{0:T(512)S(1)} %get-tuple-element.67, f32[]{:T(128)S(6)} %div.112, f32[512,1280]{1,0:T(8,128)} %copy-done), kind=kLoop, calls=%fused_computation.32 | loop fusion | flops 5242880 | bytes 11803656 | tf_op jit(solution)/shard_map/convert_element_type | solution.py:15
  263.5 0.0 all-gather.4.cloned.1.call-update
  263.5 0.0 all-gather.6.cloned.1.call-start
  264.3 6.3 %fusion.7 = (bf16[640,1024]{1,0:T(8,128)(2,1)}, f32[640,1024]{1,0:T(8,128)}, f32[640,1024]{1,0:T(8,128)}) fusion(f32[640,1024]{1,0:T(8,128)} %param.17, f32[]{:T(128)S(6)} %max.10, f32[1024]{0:T(1024)S(1)} %multiply_add_fusion.5, f32[640]{0:T(1024)S(1)} %get-tuple-element.72, f32[]{:T(128)S(6)} %div.124, f32[640,1024]{1,0:T(8,128)S(1)} %convert_reduce_fusion), kind=kLoop, calls=%fused_computation.31 | loop fusion | flops 5242880 | bytes 11803144 | tf_op jit(solution)/shard_map/convert_element_type | solution.py:15
  270.5 0.0 all-gather.6.cloned.1.call-update
  270.6 20.2 %all-gather.8.cloned.1.call-done = bf16[1024,1024]{1,0:T(8,128)(2,1)} async-done(((bf16[512,1024]{1,0:T(8,128)(2,1)}), bf16[1024,1024]{1,0:T(8,128)(2,1)}) %all-gather.8.cloned.1.call-update) | async-done | bytes 2097168 | tf_op jit(solution)/shard_map/all_gather | solution.py:15
  290.7 41.1 %all-gather.4.cloned.1.call-done = bf16[1024,1280]{1,0:T(8,128)(2,1)} async-done(((bf16[512,1280]{1,0:T(8,128)(2,1)}), bf16[1024,1280]{1,0:T(8,128)(2,1)}) %all-gather.4.cloned.1.call-update) | async-done | bytes 2621456 | tf_op jit(solution)/shard_map/all_gather | solution.py:15
  331.9 41.2 %all-gather.6.cloned.1.call-done = bf16[1280,1024]{1,0:T(8,128)(2,1)} async-done(((bf16[640,1024]{1,0:T(8,128)(2,1)}), bf16[1280,1024]{1,0:T(8,128)(2,1)}) %all-gather.6.cloned.1.call-update) | async-done | bytes 2621456 | tf_op jit(solution)/shard_map/all_gather | solution.py:15
  373.1 3.5 copy.45
  376.6 1.5 copy.46
  378.1 1.0 copy-done.6
  379.1 1.3 copy.47
  (28 shorter events, 0.1 us)
Async XLA Ops:
  29.7 5.5 %copy-start.4 = (bf16[1,1024,1280]{2,1,0:T(8,128)(2,1)S(1)}, bf16[1,1024,1280]{2,1,0:T(8,128)(2,1)}, u32[]{:S(2)}) copy-start(bf16[1,1024,1280]{2,1,0:T(8,128)(2,1)} %param.12) | copy-start | bytes 7864324
  29.7 40.3 %all-to-all-start.2 = ((bf16[2,2,262144]{2,1,0:T(2,128)(2,1)}), bf16[2,2,262144]{2,1,0:T(2,128)(2,1)}, u32[]{:S(2)}, u32[]{:S(2)}) async-start(bf16[2,2,262144]{2,1,0:T(2,128)(2,1)} %reshape.58), calls=%async_computation.2 | async-start | bytes 4194304 | tf_op jit(solution)/shard_map/all_to_all | solution.py:20
  70.0 5.8 %copy-start.5 = (bf16[1,1280,1024]{2,1,0:T(8,128)(2,1)S(1)}, bf16[1,1280,1024]{2,1,0:T(8,128)(2,1)}, u32[]{:S(2)}) copy-start(bf16[1,1280,1024]{2,1,0:T(8,128)(2,1)} %param.16) | copy-start | bytes 7864324
  70.0 42.6 %all-to-all-start = ((bf16[2,2,327680]{2,1,0:T(2,128)(2,1)}), bf16[2,2,327680]{2,1,0:T(2,128)(2,1)}, u32[]{:S(2)}, u32[]{:S(2)}) async-start(bf16[2,2,327680]{2,1,0:T(2,128)(2,1)} %reshape.54), calls=%async_computation | async-start | bytes 5242880 | tf_op jit(solution)/shard_map/all_to_all | solution.py:20
  112.6 35.7 %all-to-all-start.1 = ((bf16[2,2,327680]{2,1,0:T(2,128)(2,1)}), bf16[2,2,327680]{2,1,0:T(2,128)(2,1)S(1)}, u32[]{:S(2)}, u32[]{:S(2)}) async-start(bf16[2,2,327680]{2,1,0:T(2,128)(2,1)} %reshape.56), calls=%async_computation.1 | async-start | bytes 5242880 | tf_op jit(solution)/shard_map/all_to_all | solution.py:20
  116.8 174.0 %all-gather.8.cloned.1.call-start = ((), (), s32[]{:S(2)}) async-start(), calls=%async_computation.5 | async-start | bytes 3145728 | tf_op jit(solution)/shard_map/all_gather | solution.py:15
  124.7 1.3 copy-start.1
  134.9 1.5 copy-start
  156.2 6.8 %copy-start.14 = (f32[640]{0:T(1024)S(1)}, f32[640]{0:T(1024)}, u32[]{:S(2)}) copy-start(f32[640]{0:T(1024)} %param.18) | copy-start | bytes 7684
  156.2 7.4 %copy-start.17 = (f32[512]{0:T(512)S(1)}, f32[512]{0:T(512)}, u32[]{:S(2)}) copy-start(f32[512]{0:T(512)} %param.22) | copy-start | bytes 6148
  156.2 7.4 %copy-start.18 = (f32[512]{0:T(512)S(1)}, f32[512]{0:T(512)}, u32[]{:S(2)}) copy-start(f32[512]{0:T(512)} %param.14) | copy-start | bytes 6148
  156.2 47.3 %copy-start.13 = (f32[1280]{0:T(1024)S(1)}, f32[1280]{0:T(1024)}, u32[]{:S(2)}) copy-start(f32[1280]{0:T(1024)} %param.15) | copy-start | bytes 15364
  156.2 47.3 %copy-start.15 = (f32[1024]{0:T(1024)S(1)}, f32[1024]{0:T(1024)}, u32[]{:S(2)}) copy-start(f32[1024]{0:T(1024)} %param.19) | copy-start | bytes 12292
  156.2 48.0 %copy-start.16 = (f32[1024]{0:T(1024)S(1)}, f32[1024]{0:T(1024)}, u32[]{:S(2)}) copy-start(f32[1024]{0:T(1024)} %param.23) | copy-start | bytes 12292
  163.6 100.7 %copy-start.9 = (f32[640]{0:T(1024)}, f32[640]{0:T(1024)S(1)}, u32[]{:S(2)}) copy-start(f32[640]{0:T(1024)S(1)} %get-tuple-element.72) | copy-start | bytes 7684
  164.2 86.0 %copy-start.11 = (f32[512]{0:T(512)}, f32[512]{0:T(512)S(1)}, u32[]{:S(2)}) copy-start(f32[512]{0:T(512)S(1)} %get-tuple-element.77) | copy-start | bytes 6148
  164.2 92.6 %copy-start.12 = (f32[512]{0:T(512)}, f32[512]{0:T(512)S(1)}, u32[]{:S(2)}) copy-start(f32[512]{0:T(512)S(1)} %get-tuple-element.67) | copy-start | bytes 6148
  203.5 53.3 %copy-start.7 = (f32[1280]{0:T(1024)}, f32[1280]{0:T(1024)S(1)}, u32[]{:S(2)}) copy-start(f32[1280]{0:T(1024)S(1)} %multiply_add_fusion.3) | copy-start | bytes 15364
  203.5 60.7 %copy-start.10 = (f32[1024]{0:T(1024)}, f32[1024]{0:T(1024)S(1)}, u32[]{:S(2)}) copy-start(f32[1024]{0:T(1024)S(1)} %multiply_add_fusion.5) | copy-start | bytes 12292
  204.2 46.0 %copy-start.8 = (f32[1024]{0:T(1024)}, f32[1024]{0:T(1024)S(1)}, u32[]{:S(2)}) copy-start(f32[1024]{0:T(1024)S(1)} %multiply_add_fusion.4) | copy-start | bytes 12292
  204.2 6.1 %copy-start.2 = (f32[512,1024]{1,0:T(8,128)S(1)}, f32[512,1024]{1,0:T(8,128)}, u32[]{:S(2)}) copy-start(f32[512,1024]{1,0:T(8,128)} %copy-done.1) | copy-start | bytes 6291460
  256.1 75.8 %all-gather.4.cloned.1.call-start = ((), (), s32[]{:S(2)}) async-start(), calls=%async_computation.3 | async-start | bytes 3932160 | tf_op jit(solution)/shard_map/all_gather | solution.py:15
  263.5 109.5 %all-gather.6.cloned.1.call-start = ((), (), s32[]{:S(2)}) async-start(), calls=%async_computation.4 | async-start | bytes 3932160 | tf_op jit(solution)/shard_map/all_gather | solution.py:15
  373.1 3.6 copy-start.3
  376.6 2.5 copy-start.6
Sparse Core Ops, SparseCore 0:
  256.2 34.4 all-gather.7
  292.9 38.9 all-gather.3
  334.0 38.9 all-gather.5
where the time goes:
time: 393 us; the launch traced here: 387 us
  waiting for transfers between devices  114 us (29%)
  other arithmetic  86.1 us (22%)
  blocking collectives  81.4 us (21%)
  local copies, waits for them, and re-layouts  71.9 us (18%)
  between operations  18.3 us (5%)
  starting transfers between devices  15.7 us (4%)
    all_gather x3, waiting for transfers between devices, finish(): lax.all_gather(updated.astype(jnp.bfloat16), 'dp', axis=0, tiled=True)  102 us
    unnamed x51, local copies, waits for them, and re-layouts  62.5 us
    unnamed x3, other arithmetic  55 us
    psum x1, blocking collectives, body(): lax.psum((column_parts[which], jnp.sum(rows_next)), ('dp', 'row'))  38 us
    psum x1, blocking collectives, body(): lax.psum(jnp.sum(update_raw * update_raw), ('dp', 'row', 'col'))  37.2 us
    convert_element_type x3, other arithmetic, finish(): updated.astype(jnp.bfloat16)  18.8 us
    all_to_all x3, starting transfers between devices, reduce_gradient(): lax.all_to_all(gradient, 'dp', split_axis=1, concat_axis=0, tiled=True)  15.4 us
    all_to_all x3, waiting for transfers between devices, reduce_gradient(): lax.all_to_all(gradient, 'dp', split_axis=1, concat_axis=0, tiled=True)  11.3 us
  transfers between devices with their start and end apart: 6, of which 4 were waited for; matrix products, arithmetic and copies ran while one was open for 26% of the time, Pallas kernels for 0%

commit v1 on v0

--- a/solution.py
+++ b/solution.py
@@ -56,7 +56,9 @@
     for which in range(3):
         row_total = lax.psum(row_parts[which], "col")
         rows_next = decay_rate * groups[which][2] + (1.0 - decay_rate) * row_total / widths[which]
-        column_total, rows_sum = lax.psum((column_parts[which], jnp.sum(rows_next)), ("dp", "row"))
+        column_total, rows_sum = lax.psum(
+            lax.psum((column_parts[which], jnp.sum(rows_next)), "row"), "dp"
+        )
         columns_next = (
             decay_rate * groups[which][3] + (1.0 - decay_rate) * column_total / heights[which]
         )

time: 393 us -> 384 us (0.977)
  blocking collectives: 81.4 us -> 73.8 us
    psum x1 -> x2, blocking collectives: 38 us -> 28.8 us  [the longest x1 20.4 us: body(): lax.psum((column_parts[which], jnp.sum(rows_next)), 'row')]
  transfers between devices with their start and end apart: 6 -> 6, of which waited for: 4 -> 4; matrix products, arithmetic and copies ran while one was open for 26% -> 27% of each run, Pallas kernels for 0% -> 0%
where the time goes in v1:
time: 384 us; the launch traced here: 378 us
  waiting for transfers between devices  112 us (29%)
  other arithmetic  86 us (22%)
  blocking collectives  73.8 us (19%)
  local copies, waits for them, and re-layouts  71.9 us (19%)
  between operations  18.3 us (5%)
  starting transfers between devices  15.7 us (4%)
    all_gather x3, waiting for transfers between devices, finish(): lax.all_gather(updated.astype(jnp.bfloat16), 'dp', axis=0, tiled=True)  101 us
    unnamed x51, local copies, waits for them, and re-layouts  62.5 us
    unnamed x3, other arithmetic  55 us
    psum x1, blocking collectives, body(): lax.psum(jnp.sum(update_raw * update_raw), ('dp', 'row', 'col'))  38.8 us
    psum x1, blocking collectives, body(): lax.psum((column_parts[which], jnp.sum(rows_next)), 'row')  20.4 us
    convert_element_type x3, other arithmetic, finish(): updated.astype(jnp.bfloat16)  18.8 us
    all_to_all x3, starting transfers between devices, reduce_gradient(): lax.all_to_all(gradient, 'dp', split_axis=1, concat_axis=0, tiled=True)  15.4 us
    all_to_all x3, waiting for transfers between devices, reduce_gradient(): lax.all_to_all(gradient, 'dp', split_axis=1, concat_axis=0, tiled=True)  11.3 us
  transfers between devices with their start and end apart: 6, of which 4 were waited for; matrix products, arithmetic and copies ran while one was open for 27% of the time, Pallas kernels for 0%

profile of v1, /device:TPU:0, one launch (start us, length us, event | category | flops | bytes accessed | tf_op | source)
XLA Modules:
  0.0 378.2 jit_solution(5306693123718397553)
XLA Ops:
  7.2 6.8 %copy.41 = bf16[1,1024,1024]{2,0,1:T(2,128)(2,1)} copy(bf16[1,1024,1024]{2,1,0:T(8,128)(2,1)} %param.20) | data formatting | bytes 4194304 | tf_op args[8]
  13.9 0.5 broadcast.37
  14.4 12.8 %reduce.2 = bf16[1024,1024]{1,0:T(8,128)(2,1)S(1)} reduce(bf16[1024,1,1024]{2,1,0:T(2,128)(2,1)} %bitcast.22, bf16[]{:T(256)} %broadcast.37), dimensions={1}, to_apply=%bitcast.17.reduce_sub_computation | reduce | bytes 4194306
  27.2 2.5 reshape.58
  29.7 5.5 %all-to-all-start.2 = ((bf16[2,2,262144]{2,1,0:T(2,128)(2,1)}), bf16[2,2,262144]{2,1,0:T(2,128)(2,1)}, u32[]{:S(2)}, u32[]{:S(2)}) async-start(bf16[2,2,262144]{2,1,0:T(2,128)(2,1)} %reshape.58), calls=%async_computation.2 | async-start | bytes 4194304 | tf_op jit(solution)/shard_map/all_to_all | solution.py:20
  35.2 6.4 %copy.40 = bf16[1,1024,1280]{2,0,1:T(2,128)(2,1)} copy(bf16[1,1024,1280]{2,1,0:T(8,128)(2,1)S(1)} %copy-done.4) | data formatting | bytes 5242880 | tf_op args[0]
  41.6 26.6 %reduce = bf16[1024,1280]{1,0:T(8,128)(2,1)S(1)} reduce(bf16[1024,1,1280]{2,1,0:T(2,128)(2,1)} %bitcast.21, bf16[]{:T(256)} %broadcast.37), dimensions={1}, to_apply=%bitcast.16.reduce_sub_computation | reduce | bytes 5242882
  68.2 1.8 reshape.54
  70.0 5.8 %all-to-all-start = ((bf16[2,2,327680]{2,1,0:T(2,128)(2,1)}), bf16[2,2,327680]{2,1,0:T(2,128)(2,1)}, u32[]{:S(2)}, u32[]{:S(2)}) async-start(bf16[2,2,327680]{2,1,0:T(2,128)(2,1)} %reshape.54), calls=%async_computation | async-start | bytes 5242880 | tf_op jit(solution)/shard_map/all_to_all | solution.py:20
  75.9 18.2 %copy.39 = bf16[1,1280,1024]{2,0,1:T(2,128)(2,1)} copy(bf16[1,1280,1024]{2,1,0:T(8,128)(2,1)S(1)} %copy-done.5) | data formatting | bytes 5242880 | tf_op args[4]
  94.1 15.6 %reduce.1 = bf16[1280,1024]{1,0:T(8,128)(2,1)S(1)} reduce(bf16[1280,1,1024]{2,1,0:T(2,128)(2,1)} %bitcast.18, bf16[]{:T(256)} %broadcast.37), dimensions={1}, to_apply=%bitcast.15.reduce_sub_computation | reduce | bytes 5242882
  109.6 3.0 reshape.56
  112.6 4.1 %all-to-all-start.1 = ((bf16[2,2,327680]{2,1,0:T(2,128)(2,1)}), bf16[2,2,327680]{2,1,0:T(2,128)(2,1)S(1)}, u32[]{:S(2)}, u32[]{:S(2)}) async-start(bf16[2,2,327680]{2,1,0:T(2,128)(2,1)} %reshape.56), calls=%async_computation.1 | async-start | bytes 5242880 | tf_op jit(solution)/shard_map/all_to_all | solution.py:20
  116.8 0.2 all-gather.8.cloned.1.call-start
  116.9 4.3 %reshape.59 = bf16[1024,1,1024]{2,1,0:T(2,128)(2,1)} reshape(bf16[2,2,262144]{2,1,0:T(2,128)(2,1)} %all-to-all-done.2) | data formatting | bytes 4194304
  121.2 3.0 copy.35
  124.2 0.4 convert_reduce_fusion.2
  124.7 0.0 copy-start.1
  124.7 1.3 copy-done.1
  126.0 0.5 fusion.5
  126.5 5.1 %reshape.55 = bf16[1024,1,1280]{2,1,0:T(2,128)(2,1)} reshape(bf16[2,2,327680]{2,1,0:T(2,128)(2,1)} %all-to-all-done) | data formatting | bytes 5242880
  131.5 2.9 copy.31
  134.4 0.5 convert_reduce_fusion.1
  134.9 0.0 copy-start
  134.9 1.5 copy-done
  136.4 0.6 fusion.1
  137.0 11.3 %all-to-all-done.1 = bf16[2,2,327680]{2,1,0:T(2,128)(2,1)S(1)} async-done(((bf16[2,2,327680]{2,1,0:T(2,128)(2,1)}), bf16[2,2,327680]{2,1,0:T(2,128)(2,1)S(1)}, u32[]{:S(2)}, u32[]{:S(2)}) %all-to-all-start.1) | async-done | bytes 2621472 | tf_op jit(solution)/shard_map/all_to_all | solution.py:20
  148.3 3.7 reshape.57
  152.1 3.5 copy.33
  155.6 0.6 convert_reduce_fusion
  156.2 0.0 copy-start.14
  156.2 0.0 copy-start.17
  156.2 0.0 copy-start.18
  156.2 0.0 copy-start.13
  156.2 0.0 copy-start.15
  156.2 0.0 copy-start.16
  156.2 0.5 fusion.3
  156.8 6.2 %all-reduce.1 = (f32[512]{0:T(512)S(1)}, f32[640]{0:T(1024)S(1)}, f32[512]{0:T(512)S(1)}) all-reduce(f32[512]{0:T(512)S(1)} %get-tuple-element.17, f32[640]{0:T(1024)S(1)} %get-tuple-element.15, f32[512]{0:T(512)S(1)} %get-tuple-element.19), channel_id=1, replica_groups=mesh['dp'=2,'row'=4,'col'=4] {'col'}, use_global_device_ids=true, to_apply=%region_2.0 | all-reduce | flops 1664 | bytes 13312 | tf_op jit(solution)/shard_map/psum | solution.py:57
  163.0 0.6 fusion.10
  163.6 0.6 fusion.9
  164.2 20.4 %all-reduce.2 = (f32[1280]{0:T(1024)S(1)}, f32[]{:T(128)}, f32[1024]{0:T(1024)S(1)}, f32[]{:T(128)}, f32[1024]{0:T(1024)S(1)}, /*index=5*/f32[]{:T(128)}) all-reduce(f32[1280]{0:T(1024)S(1)} %get-tuple-element.18, f32[]{:T(128)} %get-tuple-element.54, ...), channel_id=1, replica_groups=mesh['dp'=2,'row'=4,'col'=4] {'row'}, use_global_device_ids=true, to_apply=%region_7.0 | all-reduce | flops 3331 | bytes 26648 | tf_op jit(solution)/shard_map/psum | solution.py:60
  184.6 8.3 %all-reduce.3 = (f32[1280]{0:T(1024)S(1)}, f32[]{:T(128)}, f32[1024]{0:T(1024)S(1)}, f32[]{:T(128)}, f32[1024]{0:T(1024)S(1)}, /*index=5*/f32[]{:T(128)}) all-reduce(f32[1280]{0:T(1024)S(1)} %get-tuple-element.27, f32[]{:T(128)} %get-tuple-element.28, f32[1024]{0:T(1024)S(1)} %get-tuple-element.29, ...), channel_id=1, replica_groups=mesh['dp'=2,'row'=4,'col'=4] {'dp'}, use_global_device_ids=true, to_apply=%region_8.0 | all-reduce | flops 3331 | bytes 26648 | tf_op jit(solution)/shard_map/psum | solution.py:59
  194.3 0.0 copy-start.7
  195.0 0.0 copy-start.8
  195.0 0.0 copy-start.2
  195.0 3.8 multiply_reduce_fusion.1
  198.8 2.3 multiply_reduce_fusion
  201.1 2.0 multiply_reduce_fusion.2
  203.0 38.8 %all-reduce = (f32[]{:T(128)}, f32[]{:T(128)}, f32[]{:T(128)}) all-reduce(f32[]{:T(128)} %multiply_reduce_fusion.1, f32[]{:T(128)} %multiply_reduce_fusion, f32[]{:T(128)} %multiply_reduce_fusion.2), channel_id=1, replica_groups=mesh['dp'=2,'row'=4,'col'=4] {'dp','row','col'}, use_global_device_ids=true, to_apply=%region_10.0 | all-reduce | flops 3 | bytes 24 | tf_op jit(solution)/shard_map/psum | solution.py:69
  242.6 5.9 %fusion.6 = (bf16[512,1024]{1,0:T(8,128)(2,1)}, f32[512,1024]{1,0:T(8,128)}, f32[512,1024]{1,0:T(8,128)}) fusion(f32[512,1024]{1,0:T(8,128)} %param.21, f32[]{:T(128)S(6)} %max.11, f32[1024]{0:T(1024)S(1)} %multiply_add_fusion.4, f32[512]{0:T(512)S(1)} %get-tuple-element.83, f32[]{:T(128)S(6)} %div.136, f32[512,1024]{1,0:T(8,128)} %copy-done.1), kind=kLoop, calls=%fused_computation.30 | loop fusion | flops 4194304 | bytes 9443336 | tf_op jit(solution)/shard_map/convert_element_type | solution.py:15
  248.5 0.0 all-gather.8.cloned.1.call-update
  248.5 0.0 all-gather.4.cloned.1.call-start
  249.2 6.7 %fusion.8 = (bf16[512,1280]{1,0:T(8,128)(2,1)}, f32[512,1280]{1,0:T(8,128)}, f32[512,1280]{1,0:T(8,128)}) fusion(f32[512,1280]{1,0:T(8,128)} %param.13, f32[]{:T(128)S(6)} %max.9, f32[1280]{0:T(1024)S(1)} %multiply_add_fusion.3, f32[512]{0:T(512)S(1)} %get-tuple-element.73, f32[]{:T(128)S(6)} %div.112, f32[512,1280]{1,0:T(8,128)} %copy-done), kind=kLoop, calls=%fused_computation.32 | loop fusion | flops 5242880 | bytes 11803656 | tf_op jit(solution)/shard_map/convert_element_type | solution.py:15
  255.9 0.0 all-gather.4.cloned.1.call-update
  255.9 0.0 all-gather.6.cloned.1.call-start
  256.7 6.2 %fusion.7 = (bf16[640,1024]{1,0:T(8,128)(2,1)}, f32[640,1024]{1,0:T(8,128)}, f32[640,1024]{1,0:T(8,128)}) fusion(f32[640,1024]{1,0:T(8,128)} %param.17, f32[]{:T(128)S(6)} %max.10, f32[1024]{0:T(1024)S(1)} %multiply_add_fusion.5, f32[640]{0:T(1024)S(1)} %get-tuple-element.78, f32[]{:T(128)S(6)} %div.124, f32[640,1024]{1,0:T(8,128)S(1)} %convert_reduce_fusion), kind=kLoop, calls=%fused_computation.31 | loop fusion | flops 5242880 | bytes 11803144 | tf_op jit(solution)/shard_map/convert_element_type | solution.py:15
  262.9 0.0 all-gather.6.cloned.1.call-update
  262.9 18.8 %all-gather.8.cloned.1.call-done = bf16[1024,1024]{1,0:T(8,128)(2,1)} async-done(((bf16[512,1024]{1,0:T(8,128)(2,1)}), bf16[1024,1024]{1,0:T(8,128)(2,1)}) %all-gather.8.cloned.1.call-update) | async-done | bytes 2097168 | tf_op jit(solution)/shard_map/all_gather | solution.py:15
  281.7 41.1 %all-gather.4.cloned.1.call-done = bf16[1024,1280]{1,0:T(8,128)(2,1)} async-done(((bf16[512,1280]{1,0:T(8,128)(2,1)}), bf16[1024,1280]{1,0:T(8,128)(2,1)}) %all-gather.4.cloned.1.call-update) | async-done | bytes 2621456 | tf_op jit(solution)/shard_map/all_gather | solution.py:15
  322.9 41.2 %all-gather.6.cloned.1.call-done = bf16[1280,1024]{1,0:T(8,128)(2,1)} async-done(((bf16[640,1024]{1,0:T(8,128)(2,1)}), bf16[1280,1024]{1,0:T(8,128)(2,1)}) %all-gather.6.cloned.1.call-update) | async-done | bytes 2621456 | tf_op jit(solution)/shard_map/all_gather | solution.py:15
  364.0 3.5 copy.45
  367.6 1.5 copy.46
  369.1 1.0 copy-done.6
  370.1 1.3 copy.47
  (29 shorter events, 0.1 us)
Async XLA Ops:
  29.7 5.5 %copy-start.4 = (bf16[1,1024,1280]{2,1,0:T(8,128)(2,1)S(1)}, bf16[1,1024,1280]{2,1,0:T(8,128)(2,1)}, u32[]{:S(2)}) copy-start(bf16[1,1024,1280]{2,1,0:T(8,128)(2,1)} %param.12) | copy-start | bytes 7864324
  29.7 40.3 %all-to-all-start.2 = ((bf16[2,2,262144]{2,1,0:T(2,128)(2,1)}), bf16[2,2,262144]{2,1,0:T(2,128)(2,1)}, u32[]{:S(2)}, u32[]{:S(2)}) async-start(bf16[2,2,262144]{2,1,0:T(2,128)(2,1)} %reshape.58), calls=%async_computation.2 | async-start | bytes 4194304 | tf_op jit(solution)/shard_map/all_to_all | solution.py:20
  70.0 5.8 %copy-start.5 = (bf16[1,1280,1024]{2,1,0:T(8,128)(2,1)S(1)}, bf16[1,1280,1024]{2,1,0:T(8,128)(2,1)}, u32[]{:S(2)}) copy-start(bf16[1,1280,1024]{2,1,0:T(8,128)(2,1)} %param.16) | copy-start | bytes 7864324
  70.0 42.6 %all-to-all-start = ((bf16[2,2,327680]{2,1,0:T(2,128)(2,1)}), bf16[2,2,327680]{2,1,0:T(2,128)(2,1)}, u32[]{:S(2)}, u32[]{:S(2)}) async-start(bf16[2,2,327680]{2,1,0:T(2,128)(2,1)} %reshape.54), calls=%async_computation | async-start | bytes 5242880 | tf_op jit(solution)/shard_map/all_to_all | solution.py:20
  112.6 35.7 %all-to-all-start.1 = ((bf16[2,2,327680]{2,1,0:T(2,128)(2,1)}), bf16[2,2,327680]{2,1,0:T(2,128)(2,1)S(1)}, u32[]{:S(2)}, u32[]{:S(2)}) async-start(bf16[2,2,327680]{2,1,0:T(2,128)(2,1)} %reshape.56), calls=%async_computation.1 | async-start | bytes 5242880 | tf_op jit(solution)/shard_map/all_to_all | solution.py:20
  116.8 165.0 %all-gather.8.cloned.1.call-start = ((), (), s32[]{:S(2)}) async-start(), calls=%async_computation.5 | async-start | bytes 3145728 | tf_op jit(solution)/shard_map/all_gather | solution.py:15
  124.7 1.3 copy-start.1
  134.9 1.5 copy-start
  156.2 6.8 %copy-start.14 = (f32[640]{0:T(1024)S(1)}, f32[640]{0:T(1024)}, u32[]{:S(2)}) copy-start(f32[640]{0:T(1024)} %param.18) | copy-start | bytes 7684
  156.2 7.4 %copy-start.17 = (f32[512]{0:T(512)S(1)}, f32[512]{0:T(512)}, u32[]{:S(2)}) copy-start(f32[512]{0:T(512)} %param.22) | copy-start | bytes 6148
  156.2 7.4 %copy-start.18 = (f32[512]{0:T(512)S(1)}, f32[512]{0:T(512)}, u32[]{:S(2)}) copy-start(f32[512]{0:T(512)} %param.14) | copy-start | bytes 6148
  156.2 38.1 %copy-start.13 = (f32[1280]{0:T(1024)S(1)}, f32[1280]{0:T(1024)}, u32[]{:S(2)}) copy-start(f32[1280]{0:T(1024)} %param.15) | copy-start | bytes 15364
  156.2 38.1 %copy-start.15 = (f32[1024]{0:T(1024)S(1)}, f32[1024]{0:T(1024)}, u32[]{:S(2)}) copy-start(f32[1024]{0:T(1024)} %param.19) | copy-start | bytes 12292
  156.2 38.8 %copy-start.16 = (f32[1024]{0:T(1024)S(1)}, f32[1024]{0:T(1024)}, u32[]{:S(2)}) copy-start(f32[1024]{0:T(1024)} %param.23) | copy-start | bytes 12292
  163.6 93.1 %copy-start.9 = (f32[640]{0:T(1024)}, f32[640]{0:T(1024)S(1)}, u32[]{:S(2)}) copy-start(f32[640]{0:T(1024)S(1)} %get-tuple-element.78) | copy-start | bytes 7684
  164.2 78.4 %copy-start.11 = (f32[512]{0:T(512)}, f32[512]{0:T(512)S(1)}, u32[]{:S(2)}) copy-start(f32[512]{0:T(512)S(1)} %get-tuple-element.83) | copy-start | bytes 6148
  164.2 85.0 %copy-start.12 = (f32[512]{0:T(512)}, f32[512]{0:T(512)S(1)}, u32[]{:S(2)}) copy-start(f32[512]{0:T(512)S(1)} %get-tuple-element.73) | copy-start | bytes 6148
  194.3 55.0 %copy-start.7 = (f32[1280]{0:T(1024)}, f32[1280]{0:T(1024)S(1)}, u32[]{:S(2)}) copy-start(f32[1280]{0:T(1024)S(1)} %multiply_add_fusion.3) | copy-start | bytes 15364
  194.3 62.4 %copy-start.10 = (f32[1024]{0:T(1024)}, f32[1024]{0:T(1024)S(1)}, u32[]{:S(2)}) copy-start(f32[1024]{0:T(1024)S(1)} %multiply_add_fusion.5) | copy-start | bytes 12292
  195.0 47.6 %copy-start.8 = (f32[1024]{0:T(1024)}, f32[1024]{0:T(1024)S(1)}, u32[]{:S(2)}) copy-start(f32[1024]{0:T(1024)S(1)} %multiply_add_fusion.4) | copy-start | bytes 12292
  195.0 6.1 %copy-start.2 = (f32[512,1024]{1,0:T(8,128)S(1)}, f32[512,1024]{1,0:T(8,128)}, u32[]{:S(2)}) copy-start(f32[512,1024]{1,0:T(8,128)} %copy-done.1) | copy-start | bytes 6291460
  248.5 74.4 %all-gather.4.cloned.1.call-start = ((), (), s32[]{:S(2)}) async-start(), calls=%async_computation.3 | async-start | bytes 3932160 | tf_op jit(solution)/shard_map/all_gather | solution.py:15
  255.9 108.1 %all-gather.6.cloned.1.call-start = ((), (), s32[]{:S(2)}) async-start(), calls=%async_computation.4 | async-start | bytes 3932160 | tf_op jit(solution)/shard_map/all_gather | solution.py:15
  364.0 3.6 copy-start.3
  367.6 2.5 copy-start.6
Sparse Core Ops, SparseCore 0:
  248.6 33.0 all-gather.7
  283.8 38.9 all-gather.3
  325.0 38.9 all-gather.5
